TPU v7x, 32 devices: a whole 2x2x4 slice. The times are simulated.
32 devices in a mesh: dp: 16 (over z, y, core), sp: 2 (over x).
Axes of the slice: x: 2, y: 2, z: 4, core: 2. Of those that a mesh axis runs over, the one named last changes fastest.
Arguments:
- hidden: bfloat16 [16, 4, 128, 3584], P('dp', None, 'sp'), may hold values from -6 to 6
- segment_ids: int32 [16, 4, 128], P('dp'), may hold values from -1 to 15, as said below
- w_query: bfloat16 [3584, 3584], P(None, 'sp'), may hold values from -0.10022297 to 0.10022297
- key_matrix: bfloat16 [3584, 512], P(None, 'sp'), may hold values from -0.10022297 to 0.10022297
- value_matrix: bfloat16 [3584, 512], P(None, 'sp'), may hold values from -0.10022297 to 0.10022297
Outputs:
- mixed: bfloat16 [16, 512, 3584], P('dp', 'sp')
Inputs may be any that keep to these rules, and one draw needn't show every extreme that they name: `segment_ids`: in each outbox the live slots come first; over them the ids start at 0 and never fall, by steps of 0 or 1; empty slots hold -1. Every group has an outbox whose 128 slots are all live.
All inputs are finite; a program needn't handle non-finite values.
Results may differ from a plain program's by a relative error of at most 0.0087.
Values may be sent and summed in bfloat16 or wider, within the bound.
A program may use at most 64 MiB of HBM per device.

v0:
```python
import jax
import jax.numpy as jnp
from jax import lax
from jax.sharding import PartitionSpec as P

HEAD_SIZE = 128
NSEG = 16
GROUP_SLOTS = 512


ROPE_BASE = 1000000.0


def shifted(value, axis, steps):
    count = lax.axis_size(axis)
    pairs = [(source, (source + steps) % count) for source in range(count)]
    return lax.ppermute(value, axis, pairs)


def rotate(tensor, where):
    half_width = tensor.shape[-1] // 2
    freq = ROPE_BASE ** (-(jnp.arange(half_width, dtype=jnp.float32) * 2.0 / tensor.shape[-1]))
    angle = where[:, None] * freq[None, :]
    cosine = jnp.cos(angle)[:, None, :]
    sine = jnp.sin(angle)[:, None, :]
    first = tensor[..., :half_width]
    second = tensor[..., half_width:]
    return jnp.concatenate(
        [first * cosine - second * sine, second * cosine + first * sine], axis=-1
    )


def positions(segments):
    slot_ids = jnp.arange(NSEG, dtype=jnp.int32)
    onehot = (segments[..., :, None] == slot_ids).astype(jnp.int32)
    living = (segments >= 0).astype(jnp.int32)
    below = jnp.sum(
        (segments[..., :, None] < slot_ids).astype(jnp.int32) * living[..., :, None], axis=-2
    )
    first_slot = jnp.sum(onehot * below[..., None, :], axis=-1)
    index = jnp.arange(segments.shape[-1], dtype=jnp.int32)
    return (index - first_slot).astype(jnp.float32)


def attend(queries, projected_key_rows, projected_value_rows, labels):
    total_rows = queries.shape[0]
    kv_heads = projected_key_rows.shape[1]
    queries = queries.reshape(total_rows, kv_heads, -1, queries.shape[-1])
    scores = jnp.einsum(
        "qcgd,kcd->cgqk", queries, projected_key_rows, preferred_element_type=jnp.float32
    )
    scores = scores / jnp.sqrt(jnp.float32(queries.shape[-1]))
    index = jnp.arange(total_rows, dtype=jnp.int32)
    seen = (
        (labels[:, None] == labels[None, :])
        & (labels[:, None] >= 0)
        & (index[None, :] <= index[:, None])
    )
    seen = seen | (index[:, None] == index[None, :])
    scores = jnp.where(seen, scores, -1e30)
    largest = jnp.max(scores, axis=-1, keepdims=True)
    expo = jnp.where(seen, jnp.exp(scores - largest), 0.0)
    denominator = jnp.sum(expo, axis=-1, keepdims=True)
    probs = expo.astype(jnp.bfloat16)
    summed = jnp.einsum(
        "cgqk,kcd->qcgd", probs, projected_value_rows, preferred_element_type=jnp.float32
    )
    summed = summed / jnp.transpose(denominator, (2, 0, 1, 3))
    living = (labels >= 0).astype(jnp.float32)
    return (summed.reshape(total_rows, -1) * living[:, None]).astype(jnp.bfloat16)


def local(hidden, segment_ids, w_query, key_matrix, value_matrix):
    outboxes = hidden.shape[1]
    arrivals = [(hidden[:, 0], segment_ids[:, 0])]
    for stride in range(1, outboxes):
        arrivals.append(shifted((hidden[:, stride], segment_ids[:, stride]), "dp", stride))
    tokens_in = jnp.stack([entry[0] for entry in arrivals], axis=1)
    segments = jnp.stack([entry[1] for entry in arrivals], axis=1)
    where_all = positions(segments)
    box_ids = jnp.arange(outboxes, dtype=jnp.int32)[None, :, None]
    labels = jnp.where(segments >= 0, box_ids * NSEG + segments, -1).reshape(-1)
    query_cols = w_query.shape[1]
    key_cols = key_matrix.shape[1]
    w_joined = jnp.concatenate([w_query, key_matrix, value_matrix], axis=1)
    portion = lax.all_gather(tokens_in, "sp", axis=2, tiled=True)
    width_rows = portion.shape[2]
    flat = portion.reshape(-1, portion.shape[3])
    product = jnp.dot(flat, w_joined, preferred_element_type=jnp.float32)
    where_part = where_all.reshape(-1)
    queries = rotate(
        product[:, :query_cols].reshape(flat.shape[0], -1, HEAD_SIZE), where_part
    ).astype(jnp.bfloat16)
    projected_key_rows = rotate(
        product[:, query_cols : query_cols + key_cols].reshape(flat.shape[0], -1, HEAD_SIZE),
        where_part,
    ).astype(jnp.bfloat16)
    projected_value_rows = product[:, query_cols + key_cols :].astype(jnp.bfloat16)
    joined = jnp.concatenate(
        [
            queries.reshape(flat.shape[0], -1),
            projected_key_rows.reshape(flat.shape[0], -1),
            projected_value_rows,
        ],
        axis=1,
    )
    projected = joined.reshape(1, outboxes, width_rows, -1)
    projected = projected.reshape(GROUP_SLOTS, -1)
    queries = projected[:, :query_cols].reshape(GROUP_SLOTS, -1, HEAD_SIZE)
    projected_key_rows = projected[:, query_cols : query_cols + key_cols].reshape(
        GROUP_SLOTS, -1, HEAD_SIZE
    )
    projected_value_rows = projected[:, query_cols + key_cols :].reshape(GROUP_SLOTS, -1, HEAD_SIZE)
    attended = attend(queries, projected_key_rows, projected_value_rows, labels).reshape(
        1, GROUP_SLOTS, -1
    )
    return lax.all_to_all(attended, "sp", split_axis=1, concat_axis=2, tiled=True)


def solution(mesh):
    placed = (
        P("dp", None, "sp", None),
        P("dp", None, None),
        P(None, "sp"),
        P(None, "sp"),
        P(None, "sp"),
    )
    return jax.shard_map(
        local, mesh=mesh, in_specs=placed, out_specs=P("dp", "sp", None), check_vma=False
    )
```

profile of v0, /device:TPU:0, one launch (start us, length us, event | category | flops | bytes accessed | tf_op | source)
XLA Modules:
  0.0 220.1 jit_solution(8252332415008291170)
XLA Ops:
  6.5 0.0 all-gather.2.cloned.1.call-start
  6.5 1.6 fusion.32
  8.1 0.0 copy-start.4
  8.1 0.0 copy-start.5
  8.1 2.5 %collective-permute-start.2 = (bf16[1,64,3584]{2,1,0:T(8,128)(2,1)S(1)}, bf16[1,64,3584]{2,1,0:T(8,128)(2,1)S(1)}, u32[]{:S(2)}, u32[]{:S(2)}) collective-permute-start(bf16[1,64,3584]{2,1,0:T(8,128)(2,1)S(1)} %get-tuple-element.12), channel_id=1, source_target_pairs={{0,6},{2,8},{4,10},{6,12},{8,14},{10,16},{12,18},{14,20},{16,22},{... | collective-permute-start | bytes 1376264 | tf_op jit(solution)/shard_map/ppermute | solution.py:17
  10.6 1.5 collective-permute-start.1
  12.1 0.5 collective-permute-start
  12.6 7.7 %collective-permute-done.2 = bf16[1,64,3584]{2,1,0:T(8,128)(2,1)S(1)} collective-permute-done((bf16[1,64,3584]{2,1,0:T(8,128)(2,1)S(1)}, bf16[1,64,3584]{2,1,0:T(8,128)(2,1)S(1)}, u32[]{:S(2)}, u32[]{:S(2)}) %collective-permute-start.2) | collective-permute-done | bytes 458784 | tf_op jit(solution)/shard_map/ppermute | solution.py:17
  20.2 15.2 %collective-permute-done.1 = bf16[1,64,3584]{2,1,0:T(8,128)(2,1)S(1)} collective-permute-done((bf16[1,64,3584]{2,1,0:T(8,128)(2,1)S(1)}, bf16[1,64,3584]{2,1,0:T(8,128)(2,1)S(1)}, u32[]{:S(2)}, u32[]{:S(2)}) %collective-permute-start.1) | collective-permute-done | bytes 458784 | tf_op jit(solution)/shard_map/ppermute | solution.py:17
  35.4 4.6 %collective-permute-done = bf16[1,64,3584]{2,1,0:T(8,128)(2,1)S(1)} collective-permute-done((bf16[1,64,3584]{2,1,0:T(8,128)(2,1)S(1)}, bf16[1,64,3584]{2,1,0:T(8,128)(2,1)S(1)}, u32[]{:S(2)}, u32[]{:S(2)}) %collective-permute-start) | collective-permute-done | bytes 458784 | tf_op jit(solution)/shard_map/ppermute | solution.py:17
  40.0 1.5 pad_maximum_fusion
  41.4 0.0 all-gather.2.cloned.1.call-update
  41.4 0.0 copy-done.4
  41.5 0.1 collective-permute-start.5
  41.5 0.1 collective-permute-start.4
  41.6 0.1 collective-permute-start.3
  41.7 4.6 %collective-permute-done.5 = s32[1,128]{1,0:T(1,128)S(1)} collective-permute-done((s32[1,128]{1,0:T(1,128)S(1)}, s32[1,128]{1,0:T(1,128)S(1)}, u32[]{:S(2)}, u32[]{:S(2)}) %collective-permute-start.5) | collective-permute-done | bytes 544 | tf_op jit(solution)/shard_map/ppermute | solution.py:17
  46.3 1.5 collective-permute-done.4
  47.9 0.0 collective-permute-done.3
  47.9 0.1 select_reduce_fusion.1
  48.0 0.1 select_reduce_fusion
  48.1 0.5 multiply_cosine_fusion
  48.7 0.1 copy.84
  48.8 0.1 copy.82
  49.0 0.1 add.34
  49.0 1.0 fusion.20
  50.0 40.8 %all-gather.2.cloned.1.call-done = bf16[1,4,128,3584]{3,2,1,0:T(8,128)(2,1)} async-done(((bf16[1,4,64,3584]{3,2,1,0:T(8,128)(2,1)}), bf16[1,4,128,3584]{3,2,1,0:T(8,128)(2,1)}) %all-gather.2.cloned.1.call-update) | async-done | bytes 3670032 | tf_op jit(solution)/shard_map/all_gather | solution.py:86
  90.9 0.0 copy-done.5
  90.9 13.2 %fusion.1 = f32[512,2304]{1,0:T(8,128)S(1)} fusion(bf16[512,3584]{1,0:T(8,128)(2,1)} %bitcast.96, bf16[3584,256]{1,0:T(8,128)(2,1)S(1)} %copy-done.5, bf16[3584,256]{1,0:T(8,128)(2,1)} %param.8, bf16[3584,1792]{1,0:T(8,128)(2,1)} %param.7), kind=kOutput, calls=%fused_computation.1 | convolution fusion | flops 8505262080 | bytes 24903680 | tf_op jit(solution)/shard_map/dot_general | solution.py:89
  104.1 0.0 copy-start.1
  104.1 2.2 %slice.65 = f32[512,1792]{1,0:T(8,128)} slice(f32[512,2304]{1,0:T(8,128)S(1)} %fusion.1), slice={[0:512], [0:1792]} | slice | bytes 7340032 | tf_op jit(solution)/shard_map/slice | solution.py:92
  106.3 1.0 copy-done.1
  107.3 0.8 copy.97
  108.1 5.1 %copy.85 = f32[512,1792]{0,1:T(8,128)} copy(f32[512,1792]{1,0:T(8,128)} %slice.65) | data formatting | bytes 7340032 | tf_op jit(solution)/shard_map/slice | solution.py:92
  113.2 3.9 %subtract_convert_fusion = (bf16[512,14,64]{0,2,1:T(8,128)(2,1)}, bf16[512,14,64]{0,2,1:T(8,128)(2,1)}) fusion(f32[512,14,128]{0,2,1:T(8,128)} %bitcast.77, f32[512,64]{0,1:T(8,128)S(1)} %get-tuple-element.19, f32[512,64]{0,1:T(8,128)S(1)} %get-tuple-element.18), kind=kLoop, calls=%fused_computation.23 | loop fusion | flops 3670016 | bytes 5767168 | tf_op jit(solution)/shard_map/convert.3
  117.1 0.0 slice-start
  117.1 2.0 copy.87
  119.1 2.6 %copy.86 = bf16[512,14,64]{2,0,1:T(8,128)(2,1)} copy(bf16[512,14,64]{0,2,1:T(8,128)(2,1)} %get-tuple-element.8) | data formatting | bytes 1835008 | tf_op jit(solution)/shard_map/convert.3
  121.7 0.0 slice-done
  121.7 0.3 reshape.310
  122.0 0.0 copy-start
  122.0 0.6 fusion.33
  122.6 0.1 subtract_convert_fusion.1
  122.7 0.7 copy-done
  123.5 0.0 copy-start.2
  123.5 7.4 %fusion.15 = f32[2,512,512,7]{2,1,3,0:T(8,128)} fusion(bf16[512,2,7,64]{3,0,2,1:T(8,128)(2,1)S(1)} %bitcast.80, bf16[512,2,7,64]{3,0,2,1:T(8,128)(2,1)S(1)} %bitcast.81, bf16[512,2,64]{2,0,1:T(8,128)(2,1)S(1)} %get-tuple-element.15, bf16[512,2,64]{2,0,1:T(8,128)(2,1)S(1)} %get-tuple-element.14), kind=kOutput, calls=%fused_computation.18 | convolution fusion | flops 943718400 | bytes 16777216 | tf_op jit(solution)/shard_map/qcgd,kcd->cgqk/dot_general | solution.py:49
  130.8 0.0 copy-done.2
  130.8 0.0 copy-start.3
  130.8 13.6 %fusion.35 = (f32[2,7,512]{2,1,0:T(8,128)S(1)}, bf16[2,7,512,512]{2,3,1,0:T(8,128)(2,1)S(1)}) fusion(f32[2,512,512,7]{2,1,3,0:T(8,128)} %fusion.15, pred[512,512]{0,1:T(8,128)(4,1)S(1)} %copy-done.2), kind=kOutput, calls=%fused_computation.66 | output fusion | flops 29360640 | bytes 22310912 | tf_op jit(solution)/shard_map/sub | solution.py:62
  144.5 0.0 copy-done.3
  144.5 2.9 %bitcast_divide_fusion = f32[512,2,7,128]{0,3,2,1:T(8,128)} fusion(bf16[512,2,128,1]{0,2,3,1:T(8,128)(2,1)S(1)} %bitcast.88, bf16[2,7,512,512]{2,3,1,0:T(8,128)(2,1)S(1)} %get-tuple-element.26, f32[512,2,7]{0,2,1:T(8,128)S(1)} %bitcast.97), kind=kOutput, calls=%fused_computation.15 | convolution fusion | flops 940441600 | bytes 11300864 | tf_op jit(solution)/shard_map/cgqk,kcd->qcgd/dot_general | solution.py:65
  147.5 5.1 %copy.90 = f32[1,512,1792]{2,1,0:T(8,128)} copy(f32[1,512,1792]{1,2,0:T(8,128)} %bitcast.84) | data formatting | bytes 7340032 | tf_op jit(solution)/shard_map/reshape | solution.py:70
  152.6 2.3 %multiply_convert_fusion = bf16[1,512,1792]{2,1,0:T(8,128)(2,1)S(1)} fusion(f32[1,512,1792]{2,1,0:T(8,128)} %copy.90, f32[512]{0:T(512)S(1)} %get-tuple-element.5), kind=kLoop, calls=%fused_computation.16 | loop fusion | flops 1835008 | bytes 5507072 | tf_op jit(solution)/shard_map/convert_element_type | solution.py:70
  154.9 4.6 %copy.106 = bf16[1,512,1792]{2,0,1:T(2,128)(2,1)} copy(bf16[1,512,1792]{2,1,0:T(8,128)(2,1)S(1)} %multiply_convert_fusion) | data formatting | bytes 3670016 | tf_op jit(solution)/shard_map/convert_element_type | solution.py:70
  159.5 0.5 broadcast.216
  160.0 13.1 %reduce.2 = bf16[512,1792]{1,0:T(8,128)(2,1)} reduce(bf16[512,1,1792]{2,1,0:T(2,128)(2,1)} %bitcast.78, bf16[]{:T(256)} %broadcast.216), dimensions={1}, to_apply=%bitcast.76.reduce_sub_computation | reduce | bytes 3670018
  173.1 1.7 reshape.315
  174.8 25.5 %all_to_all.18 = bf16[2,2,229376]{2,1,0:T(2,128)(2,1)} all-to-all(bf16[2,2,229376]{2,1,0:T(2,128)(2,1)S(1)} %reshape.315), channel_id=1, replica_groups=mesh['dp'=16,'sp'=2] {'sp'}, dimensions={0} | all-to-all | bytes 3670016 | tf_op jit(solution)/shard_map/all_to_all | solution.py:117
  200.3 4.0 %reshape.316 = bf16[512,1,1792]{2,1,0:T(2,128)(2,1)} reshape(bf16[2,2,229376]{2,1,0:T(2,128)(2,1)} %all_to_all.18) | data formatting | bytes 3670016
  204.3 3.5 %copy.98 = bf16[1,512,1792]{2,1,0:T(8,128)(2,1)} copy(bf16[1,512,1792]{2,0,1:T(2,128)(2,1)} %bitcast.79) | data formatting | bytes 3670016
  207.8 2.8 %copy.92 = bf16[1,256,2,1792]{1,3,2,0:T(8,128)(2,1)S(1)} copy(bf16[1,256,2,1792]{3,1,2,0:T(8,128)(2,1)} %bitcast.83) | data formatting | bytes 3670016 | tf_op jit(solution)/shard_map/all_to_all | solution.py:117
  210.6 2.6 %copy.93 = bf16[1,256,3584]{2,1,0:T(8,128)(2,1)} copy(bf16[1,256,3584]{1,2,0:T(8,128)(2,1)S(1)} %bitcast.82) | data formatting | bytes 3670016 | tf_op jit(solution)/shard_map/all_to_all | solution.py:117
  (8 shorter events, 0.1 us)
Async XLA Ops:
  6.5 84.3 %all-gather.2.cloned.1.call-start = ((), (), s32[]{:S(2)}) async-start(), calls=%async_computation.1 | async-start | bytes 5505024 | tf_op jit(solution)/shard_map/all_gather | solution.py:86
  8.1 33.4 %copy-start.4 = (s32[1,4,128]{2,1,0:T(4,128)S(1)}, s32[1,4,128]{2,1,0:T(4,128)}, u32[]{:S(2)}) copy-start(s32[1,4,128]{2,1,0:T(4,128)} %param.6) | copy-start | bytes 6148
  8.1 82.8 %copy-start.5 = (bf16[3584,256]{1,0:T(8,128)(2,1)S(1)}, bf16[3584,256]{1,0:T(8,128)(2,1)}, u32[]{:S(2)}) copy-start(bf16[3584,256]{1,0:T(8,128)(2,1)} %param.9) | copy-start | bytes 5505028
  8.1 12.1 %collective-permute-start.2 = (bf16[1,64,3584]{2,1,0:T(8,128)(2,1)S(1)}, bf16[1,64,3584]{2,1,0:T(8,128)(2,1)S(1)}, u32[]{:S(2)}, u32[]{:S(2)}) collective-permute-start(bf16[1,64,3584]{2,1,0:T(8,128)(2,1)S(1)} %get-tuple-element.12), channel_id=1, source_target_pairs={{0,6},{2,8},{4,10},{6,12},{8,14},{10,16},{12,18},{14,20},{16,22},{... | collective-permute-start | bytes 1376264 | tf_op jit(solution)/shard_map/ppermute | solution.py:17
  10.6 24.8 %collective-permute-start.1 = (bf16[1,64,3584]{2,1,0:T(8,128)(2,1)S(1)}, bf16[1,64,3584]{2,1,0:T(8,128)(2,1)S(1)}, u32[]{:S(2)}, u32[]{:S(2)}) collective-permute-start(bf16[1,64,3584]{2,1,0:T(8,128)(2,1)S(1)} %get-tuple-element.13), channel_id=1, source_target_pairs={{0,4},{2,6},{4,8},{6,10},{8,12},{10,14},{12,16},{14,18},{16,20},{1... | collective-permute-start | bytes 1376264 | tf_op jit(solution)/shard_map/ppermute | solution.py:17
  12.1 27.8 %collective-permute-start = (bf16[1,64,3584]{2,1,0:T(8,128)(2,1)S(1)}, bf16[1,64,3584]{2,1,0:T(8,128)(2,1)S(1)}, u32[]{:S(2)}, u32[]{:S(2)}) collective-permute-start(bf16[1,64,3584]{2,1,0:T(8,128)(2,1)S(1)} %get-tuple-element.11), channel_id=1, source_target_pairs={{0,2},{2,4},{4,6},{6,8},{8,10},{10,12},{12,14},{14,16},{16,18},{18... | collective-permute-start | bytes 1376264 | tf_op jit(solution)/shard_map/ppermute | solution.py:17
  41.5 4.8 %collective-permute-start.5 = (s32[1,128]{1,0:T(1,128)S(1)}, s32[1,128]{1,0:T(1,128)S(1)}, u32[]{:S(2)}, u32[]{:S(2)}) collective-permute-start(s32[1,128]{1,0:T(1,128)S(1)} %get-tuple-element.23), channel_id=1, source_target_pairs={{0,6},{2,8},{4,10},{6,12},{8,14},{10,16},{12,18},{14,20},{16,22},{... | collective-permute-start | bytes 1544 | tf_op jit(solution)/shard_map/ppermute | solution.py:17
  41.5 6.3 %collective-permute-start.4 = (s32[1,128]{1,0:T(1,128)S(1)}, s32[1,128]{1,0:T(1,128)S(1)}, u32[]{:S(2)}, u32[]{:S(2)}) collective-permute-start(s32[1,128]{1,0:T(1,128)S(1)} %get-tuple-element.24), channel_id=1, source_target_pairs={{0,4},{2,6},{4,8},{6,10},{8,12},{10,14},{12,16},{14,18},{16,20},{1... | collective-permute-start | bytes 1544 | tf_op jit(solution)/shard_map/ppermute | solution.py:17
  41.6 6.3 %collective-permute-start.3 = (s32[1,128]{1,0:T(1,128)S(1)}, s32[1,128]{1,0:T(1,128)S(1)}, u32[]{:S(2)}, u32[]{:S(2)}) collective-permute-start(s32[1,128]{1,0:T(1,128)S(1)} %get-tuple-element.22), channel_id=1, source_target_pairs={{0,2},{2,4},{4,6},{6,8},{8,10},{10,12},{12,14},{14,16},{16,18},{18... | collective-permute-start | bytes 1544 | tf_op jit(solution)/shard_map/ppermute | solution.py:17
  104.1 3.2 %copy-start.1 = (f32[512,2304]{1,0:T(8,128)}, f32[512,2304]{1,0:T(8,128)S(1)}, u32[]{:S(2)}) copy-start(f32[512,2304]{1,0:T(8,128)S(1)} %fusion.1) | copy-start | bytes 14155780
  117.1 4.5 %slice-start = ((f32[512,2304]{1,0:T(8,128)}), f32[512,256]{1,0:T(8,128)S(1)}, s32[]{:S(2)}) async-start(f32[512,2304]{1,0:T(8,128)} %copy-done.1), calls=%async_computation.2 | async-start | bytes 1048576 | tf_op jit(solution)/shard_map/slice | solution.py:95
  122.0 1.5 copy-start
  123.5 7.4 %copy-start.2 = (pred[512,512]{0,1:T(8,128)(4,1)S(1)}, pred[512,512]{0,1:T(8,128)(4,1)}, u32[]{:S(2)}) copy-start(pred[512,512]{0,1:T(8,128)(4,1)} %fusion.20) | copy-start | bytes 786436
  130.8 13.7 %copy-start.3 = (bf16[512,256]{0,1:T(8,128)(2,1)S(1)}, bf16[512,256]{0,1:T(8,128)(2,1)}, u32[]{:S(2)}) copy-start(bf16[512,256]{0,1:T(8,128)(2,1)} %copy.97) | copy-start | bytes 786436
Sparse Core Ops, SparseCore 0:
  41.6 49.2 all-gather.1
where the time goes:
time: 221 us; the launch traced here: 220 us
  waiting for transfers between devices  74.4 us (34%)
  local copies, waits for them, and re-layouts  42.1 us (19%)
  other arithmetic  36.4 us (16%)
  blocking collectives  25.5 us (12%)
  matrix products  23.5 us (11%)
  between operations  13.6 us (6%)
  starting transfers between devices  4.64 us (2%)
    all_gather x1, waiting for transfers between devices, local(): portion = lax.all_gather(tokens_in, 'sp', axis=2, tiled=True)  40.8 us
    ppermute x6, waiting for transfers between devices, shifted(): return lax.ppermute(value, axis, pairs)  33.5 us
    all_to_all x1, blocking collectives, local(): lax.all_to_all(attended, 'sp', split_axis=1, concat_axis=2, tiled=True)  25.5 us
    sub x1, other arithmetic, attend(): expo = jnp.where(seen, jnp.exp(scores - largest), 0.0)  13.6 us
    dot_general x1, matrix products, local(): product = jnp.dot(flat, w_joined, preferred_element_type=jnp.float32)  13.2 us
    unnamed x1, other arithmetic  13.1 us
    unnamed x16, local copies, waits for them, and re-layouts  11.4 us
    dot_general x1, matrix products, attend(): jnp.einsum('qcgd,kcd->cgqk', queries, projected_key_rows, preferred_eleme...  7.37 us
  transfers between devices with their start and end apart: 7, of which 6 were waited for; matrix products, arithmetic and copies ran while one was open for 1% of the time, Pallas kernels for 0%

commit v1 on v0

v1 whole, which is shorter than its diff:
```python
import functools

import jax
import jax.numpy as jnp
from jax import lax
from jax.experimental import pallas as pl
from jax.experimental.pallas import tpu as pltpu
from jax.sharding import PartitionSpec as P

HEAD = 128
ROPE_BASE = 1000000.0
MESH = pl.DeviceIdType.MESH


def kernel(
    n_dp, n_sp, heads_per_kv, chunk,
    hidden, segs, freq, w_query, w_key, w_value, out,
    wbuf, tok, segbuf, qkv, att, cos_ref, sin_ref, bias_ref, live_ref,
    w_sem, own_sem, dp_send, dp_recv, seg_send, seg_recv, x_send, x_recv,
    o_send, o_recv,
):
    boxes = hidden.shape[1]
    slots = segs.shape[2]
    kv_cols, q_cols = w_key.shape[1], w_query.shape[1]
    n_kv = kv_cols // HEAD
    per = chunk // HEAD
    kv_chunks, q_chunks = kv_cols // chunk, q_cols // chunk
    boxes_per = boxes // n_sp
    p = lax.axis_index("dp")
    s = lax.axis_index("sp")

    def order_of(receiver, i):
        if n_sp == 2 and boxes == 4:
            mid = i + 1 - receiver
            last = 1 + 2 * receiver
            if isinstance(i, int):
                if i == 0:
                    return 0
                return last if i == boxes - 1 else mid
            return jnp.where(i == 0, 0, jnp.where(i == boxes - 1, last, mid))
        return i

    def own_order(i):
        return order_of(s, i)

    def forward_order(i):
        return order_of(n_sp - 1 - s, i)

    def weight_copy(c):
        if c < kv_chunks:
            src = w_key.at[:, pl.ds(c * chunk, chunk)]
        elif c < kv_chunks + q_chunks:
            src = w_query.at[:, pl.ds((c - kv_chunks) * chunk, chunk)]
        else:
            src = w_value.at[:, pl.ds((c - kv_chunks - q_chunks) * chunk, chunk)]
        return pltpu.make_async_copy(src, wbuf.at[c], w_sem.at[c])

    def dp_copy(j):
        return pltpu.make_async_remote_copy(
            src_ref=hidden.at[0, j], dst_ref=tok.at[j, s],
            send_sem=dp_send.at[j], recv_sem=dp_recv.at[j],
            device_id=(lax.rem(p + j, n_dp), s), device_id_type=MESH,
        )

    def seg_copy(j):
        return pltpu.make_async_remote_copy(
            src_ref=segs.at[0], dst_ref=segbuf.at[j],
            send_sem=seg_send.at[j], recv_sem=seg_recv.at[j],
            device_id=(lax.rem(p + j, n_dp), s), device_id_type=MESH,
        )

    def x_copy(src, j, k):
        return pltpu.make_async_remote_copy(
            src_ref=src, dst_ref=tok.at[j, s],
            send_sem=x_send.at[j, k - 1], recv_sem=x_recv.at[j, k - 1],
            device_id=(p, lax.rem(s + k, n_sp)), device_id_type=MESH,
        )

    own_copy = pltpu.make_async_copy(hidden.at[0, 0], tok.at[0, s], own_sem)

    barrier = pltpu.get_barrier_semaphore()
    for j in range(1, boxes):
        for q in (lax.rem(p + j, n_dp), lax.rem(p + n_dp - j, n_dp)):
            pl.semaphore_signal(barrier, inc=1, device_id=(q, s), device_id_type=MESH)
    for k in range(1, n_sp):
        pl.semaphore_signal(
            barrier, inc=1, device_id=(p, lax.rem(s + k, n_sp)), device_id_type=MESH
        )
    own_copy.start()
    pl.semaphore_wait(barrier, 2 * (boxes - 1) + n_sp - 1)

    for k in range(1, n_sp):
        x_copy(hidden.at[0, 0], 0, k).start()
    for j in range(1, boxes):
        seg_copy(j).start()
    for i in range(1, boxes):
        dp_copy(forward_order(i)).start()
    total_chunks = 2 * kv_chunks + q_chunks
    for c in range(total_chunks):
        weight_copy(c).start()

    segbuf[0] = segs[0]
    own_copy.wait()
    for j in range(1, boxes):
        seg_copy(j).wait()

    def forward(i):
        j = forward_order(i)
        dp_copy(j).wait_recv()
        for k in range(1, n_sp):
            x_copy(tok.at[j, s], j, k).start()

    def out_slice(j):
        row = pl.multiple_of(lax.rem(j, boxes_per) * slots, slots)
        col = pl.multiple_of(s * q_cols, HEAD)
        return out.at[0, pl.ds(row, slots), pl.ds(col, q_cols)]

    def local_out(i, j):
        return pltpu.make_async_copy(att.at[i], out_slice(j), o_send.at[i])

    def remote_out(i, j):
        owner = j // boxes_per
        k = lax.rem(owner - s + n_sp, n_sp)
        return pltpu.make_async_remote_copy(
            src_ref=att.at[i], dst_ref=out_slice(j),
            send_sem=o_send.at[i], recv_sem=o_recv.at[lax.rem(j, boxes_per), k - 1],
            device_id=(p, owner), device_id_type=MESH,
        )

    def tables(j):
        box = segbuf[j].astype(jnp.float32)
        pick = lax.broadcasted_iota(jnp.int32, box.shape, 0) == j
        row = jnp.sum(jnp.where(pick, box, 0.0), axis=0, keepdims=True)
        r = lax.broadcasted_iota(jnp.int32, (slots, slots), 0)
        c = lax.broadcasted_iota(jnp.int32, (slots, slots), 1)
        row = jnp.broadcast_to(row, (slots, slots))
        col = jnp.sum(jnp.where(r == c, row, 0.0), axis=1, keepdims=True)
        below = jnp.sum(
            jnp.where((row < col) & (row >= 0.0), 1.0, 0.0), axis=1, keepdims=True
        )
        where = r[:, :1].astype(jnp.float32) - below
        angle = where * freq[0:1, :]
        lane = lax.broadcasted_iota(jnp.int32, angle.shape, 1)
        cos_ref[...] = jnp.cos(angle)
        sine = jnp.sin(angle)
        sin_ref[...] = jnp.where(lane < HEAD // 2, -sine, sine)
        seen = ((row == col) & (col >= 0.0) & (c <= r)) | (c == r)
        bias_ref[...] = jnp.where(seen, 0.0, -1e30)
        live_ref[...] = jnp.broadcast_to(
            jnp.where(col >= 0.0, 1.0, 0.0), (slots, HEAD)
        )

    def step(i, carry):
        j = own_order(i)
        tables(j)

        @pl.when(i == 0)
        def _():
            forward(1)

        @pl.when(i == 1)
        def _():
            for later in range(2, boxes):
                forward(later)

        for k in range(1, n_sp):
            source = lax.rem(s + n_sp - k, n_sp)
            pltpu.make_async_remote_copy(
                src_ref=tok.at[j, source], dst_ref=tok.at[j, source],
                send_sem=x_send.at[j, k - 1], recv_sem=x_recv.at[j, k - 1],
                device_id=(p, lax.rem(s + k, n_sp)), device_id_type=MESH,
            ).wait_recv()

        def project(c):
            @pl.when(i == 0)
            def _():
                pltpu.make_async_copy(wbuf.at[c], wbuf.at[c], w_sem.at[c]).wait()

            x = tok[j].reshape(slots, tok.shape[3])
            return jnp.dot(x, wbuf[c], preferred_element_type=jnp.float32)

        def rotated(c, carry):
            prod = project(c)
            for h in range(per):
                t = prod[:, h * HEAD : (h + 1) * HEAD]
                turned = pltpu.roll(t, HEAD // 2, 1)
                qkv[c * per + h] = (t * cos_ref[...] + turned * sin_ref[...]).astype(
                    jnp.bfloat16
                )
            return carry

        lax.fori_loop(0, kv_chunks + q_chunks, rotated, 0)
        for c in range(kv_chunks + q_chunks, total_chunks):
            prod = project(c)
            for h in range(per):
                qkv[c * per + h] = prod[:, h * HEAD : (h + 1) * HEAD].astype(jnp.bfloat16)

        scale = 1.0 / (HEAD ** 0.5)
        bias = bias_ref[...]
        live = live_ref[...]
        v_base = n_kv + n_kv * heads_per_kv
        for g in range(n_kv):
            keys = qkv[g]
            values = qkv[v_base + g]
            for h in range(heads_per_kv):
                head = g * heads_per_kv + h
                scores = lax.dot_general(
                    qkv[n_kv + head], keys, (((1,), (1,)), ((), ())),
                    preferred_element_type=jnp.float32,
                )
                scores = scores * scale + bias
                top = jnp.max(scores, axis=1, keepdims=True)
                e = jnp.exp(scores - top)
                total = jnp.sum(e, axis=1, keepdims=True)
                mixed = jnp.dot(
                    e.astype(jnp.bfloat16), values, preferred_element_type=jnp.float32
                )
                att[i, :, head * HEAD : (head + 1) * HEAD] = (
                    mixed / total * live
                ).astype(jnp.bfloat16)

        @pl.when(j // boxes_per == s)
        def _():
            local_out(i, j).start()

        @pl.when(j // boxes_per != s)
        def _():
            remote_out(i, j).start()

        return carry

    lax.fori_loop(0, boxes, step, 0)

    for j in range(1, boxes):
        dp_copy(j).wait_send()
    for j in range(boxes):
        for k in range(1, n_sp):
            x_copy(tok.at[j, s], j, k).wait_send()
    for i in range(boxes):
        j = own_order(i)

        @pl.when(j // boxes_per == s)
        def _():
            local_out(i, j).wait()

        @pl.when(j // boxes_per != s)
        def _():
            remote_out(i, j).wait_send()

    for b in range(boxes_per):
        for k in range(1, n_sp):
            source = lax.rem(s + n_sp - k, n_sp)
            dst = out.at[
                0, pl.ds(b * slots, slots),
                pl.ds(pl.multiple_of(source * q_cols, HEAD), q_cols),
            ]
            pltpu.make_async_remote_copy(
                src_ref=att.at[0], dst_ref=dst,
                send_sem=o_send.at[0], recv_sem=o_recv.at[b, k - 1],
                device_id=(p, source), device_id_type=MESH,
            ).wait_recv()


def solution(mesh):
    n_dp, n_sp = mesh.shape["dp"], mesh.shape["sp"]

    def local(hidden, segment_ids, w_query, key_matrix, value_matrix):
        boxes, part, width = hidden.shape[1:]
        slots = segment_ids.shape[2]
        q_cols, kv_cols = w_query.shape[1], key_matrix.shape[1]
        chunk = 2 * HEAD if kv_cols % (2 * HEAD) == 0 and q_cols % (2 * HEAD) == 0 else HEAD
        chunks = (q_cols + 2 * kv_cols) // chunk
        heads = (q_cols + 2 * kv_cols) // HEAD
        half = jnp.arange(HEAD // 2, dtype=jnp.float32)
        freq = ROPE_BASE ** (-(half * 2.0 / HEAD))
        freq = jnp.broadcast_to(jnp.concatenate([freq, freq])[None, :], (8, HEAD))
        vmem = pl.BlockSpec(memory_space=pltpu.VMEM)
        hbm = pl.BlockSpec(memory_space=pl.ANY)
        dma = pltpu.SemaphoreType.DMA
        return pl.pallas_call(
            functools.partial(kernel, n_dp, n_sp, q_cols // kv_cols, chunk),
            out_shape=jax.ShapeDtypeStruct(
                (1, boxes * slots // n_sp, q_cols * n_sp), jnp.bfloat16
            ),
            in_specs=[hbm, vmem, vmem, hbm, hbm, hbm],
            out_specs=hbm,
            scratch_shapes=[
                pltpu.VMEM((chunks, width, chunk), jnp.bfloat16),
                pltpu.VMEM((boxes, n_sp, part, width), jnp.bfloat16),
                pltpu.VMEM((boxes, boxes, slots), jnp.int32),
                pltpu.VMEM((heads, slots, HEAD), jnp.bfloat16),
                pltpu.VMEM((boxes, slots, q_cols), jnp.bfloat16),
                pltpu.VMEM((slots, HEAD), jnp.float32),
                pltpu.VMEM((slots, HEAD), jnp.float32),
                pltpu.VMEM((slots, slots), jnp.float32),
                pltpu.VMEM((slots, HEAD), jnp.float32),
                dma((chunks,)),
                dma,
                dma((boxes,)),
                dma((boxes,)),
                dma((boxes,)),
                dma((boxes,)),
                dma((boxes, n_sp - 1)),
                dma((boxes, n_sp - 1)),
                dma((boxes,)),
                dma((boxes // n_sp, n_sp - 1)),
            ],
            compiler_params=pltpu.CompilerParams(
                collective_id=0, has_side_effects=True, vmem_limit_bytes=60 * 1024 * 1024
            ),
            name="rebalanced_attention",
        )(hidden, segment_ids, freq, w_query, key_matrix, value_matrix)

    placed = (
        P("dp", None, "sp", None),
        P("dp", None, None),
        P(None, "sp"),
        P(None, "sp"),
        P(None, "sp"),
    )
    return jax.shard_map(
        local, mesh=mesh, in_specs=placed, out_specs=P("dp", "sp", None), check_vma=False
    )
```

time: 221 us -> 73.7 us (0.33)
  waiting for transfers between devices: 74.4 us -> 0 us
  Pallas kernels: 0 us -> 69.9 us
  local copies, waits for them, and re-layouts: 42.1 us -> 3.45 us
  other arithmetic: 36.4 us -> 0.09 us
  blocking collectives: 25.5 us -> 0 us
  matrix products: 23.5 us -> 0 us
  between operations: 13.6 us -> 0.01 us
  starting transfers between devices: 4.64 us -> 0 us
    pallas_call x0 -> x1, Pallas kernels: none -> 69.9 us  [local(): pl.pallas_call(functools.partial(kernel, n_dp, n_sp, q_cols // kv_cols, c...]
    all_gather x1 -> x0, waiting for transfers between devices: 40.8 us -> none  [local(): portion = lax.all_gather(tokens_in, 'sp', axis=2, tiled=True)]
    ppermute x6 -> x0, waiting for transfers between devices: 33.5 us -> none  [shifted(): return lax.ppermute(value, axis, pairs)]
    all_to_all x1 -> x0, blocking collectives: 25.5 us -> none  [local(): lax.all_to_all(attended, 'sp', split_axis=1, concat_axis=2, tiled=True)]
    dot_general x3 -> x0, matrix products: 23.5 us -> none  [the longest x1 13.2 us: local(): product = jnp.dot(flat, w_joined, preferred_element_type=jnp.float32)]
    sub x1 -> x0, other arithmetic: 13.6 us -> none  [attend(): expo = jnp.where(seen, jnp.exp(scores - largest), 0.0)]
    unnamed x1 -> x0, other arithmetic: 13.1 us -> none
    slice x8 -> x0, local copies, waits for them, and re-layouts: 9.52 us -> none  [the longest x2 7.33 us: local(): product[:, :query_cols].reshape(flat.shape[0], -1, HEAD_SIZE)]
  transfers between devices with their start and end apart: 7 -> 0, of which waited for: 6 -> 0; matrix products, arithmetic and copies ran while one was open for 1% -> 0% of each run, Pallas kernels for 0% -> 0%
where the time goes in v1:
time: 73.7 us; the launch traced here: 73.5 us
  Pallas kernels  69.9 us (95%)
  local copies, waits for them, and re-layouts  3.45 us (5%)
    pallas_call x1, Pallas kernels, local(): pl.pallas_call(functools.partial(kernel, n_dp, n_sp, q_cols // kv_cols, c...  69.9 us
    unnamed x1, local copies, waits for them, and re-layouts  2.85 us

profile of v1, /device:TPU:0, one launch (start us, length us, event | category | flops | bytes accessed | tf_op | source)
XLA Modules:
  0.0 73.5 jit_solution(5562006812399253216)
XLA Ops:
  0.0 0.1 pad_maximum_fusion
  0.1 0.6 broadcast_in_dim.2.freq
  0.7 69.9 %rebalanced_attention.1 = bf16[1,256,3584]{2,1,0:T(8,128)(2,1)} custom-call(bf16[1,4,64,3584]{3,2,1,0:T(8,128)(2,1)} %hidden.1, s32[1,4,128]{2,1,0:T(4,128)} %segs.1, f32[8,128]{1,0:T(8,128)} %broadcast_in_dim.2.freq, bf16[3584,1792]{1,0:T(8,128)(2,1)} %w_query.1, bf16[3584,256]{1,0:T(8,128)(2,1)} %w_key.1, bf16[3584,256]{1,0:T(8,128)(2,1)} %w_value.1), custom_call_target="tpu_custom_call" | custom-call | tf_op jit(solution)/shard_map/rebalanced_attention/pallas_call | solution.py:280
  70.6 2.8 %copy.7 = bf16[1,256,3584]{2,1,0:T(8,128)(2,1)} copy(bf16[1,256,3584]{2,1,0:T(8,128)(2,1)} %rebalanced_attention.1) | data formatting | bytes 3670016
  (1 shorter events, 0.0 us)

commit v2 on v1

--- a/solution.py
+++ b/solution.py
@@ -2,6 +2,7 @@
 
 import jax
 import jax.numpy as jnp
+import numpy as np
 from jax import lax
 from jax.experimental import pallas as pl
 from jax.experimental.pallas import tpu as pltpu
@@ -9,6 +10,7 @@
 
 HEAD = 128
 ROPE_BASE = 1000000.0
+PIECES = 2
 MESH = pl.DeviceIdType.MESH
 
 
@@ -55,10 +57,15 @@
             src = w_value.at[:, pl.ds((c - kv_chunks - q_chunks) * chunk, chunk)]
         return pltpu.make_async_copy(src, wbuf.at[c], w_sem.at[c])
 
-    def dp_copy(j):
+    rows = hidden.shape[2] // PIECES
+
+    def piece(ref, h):
+        return ref.at[pl.ds(h * rows, rows)]
+
+    def dp_copy(j, h):
         return pltpu.make_async_remote_copy(
-            src_ref=hidden.at[0, j], dst_ref=tok.at[j, s],
-            send_sem=dp_send.at[j], recv_sem=dp_recv.at[j],
+            src_ref=piece(hidden.at[0, j], h), dst_ref=piece(tok.at[j, s], h),
+            send_sem=dp_send.at[j, h], recv_sem=dp_recv.at[j, h],
             device_id=(lax.rem(p + j, n_dp), s), device_id_type=MESH,
         )
 
@@ -69,10 +76,10 @@
             device_id=(lax.rem(p + j, n_dp), s), device_id_type=MESH,
         )
 
-    def x_copy(src, j, k):
+    def x_copy(src, j, k, h):
         return pltpu.make_async_remote_copy(
-            src_ref=src, dst_ref=tok.at[j, s],
-            send_sem=x_send.at[j, k - 1], recv_sem=x_recv.at[j, k - 1],
+            src_ref=piece(src, h), dst_ref=piece(tok.at[j, s], h),
+            send_sem=x_send.at[j, k - 1, h], recv_sem=x_recv.at[j, k - 1, h],
             device_id=(p, lax.rem(s + k, n_sp)), device_id_type=MESH,
         )
 
@@ -89,12 +96,14 @@
     own_copy.start()
     pl.semaphore_wait(barrier, 2 * (boxes - 1) + n_sp - 1)
 
-    for k in range(1, n_sp):
-        x_copy(hidden.at[0, 0], 0, k).start()
     for j in range(1, boxes):
         seg_copy(j).start()
+    for h in range(PIECES):
+        for k in range(1, n_sp):
+            x_copy(hidden.at[0, 0], 0, k, h).start()
     for i in range(1, boxes):
-        dp_copy(forward_order(i)).start()
+        for h in range(PIECES):
+            dp_copy(forward_order(i), h).start()
     total_chunks = 2 * kv_chunks + q_chunks
     for c in range(total_chunks):
         weight_copy(c).start()
@@ -106,9 +115,10 @@
 
     def forward(i):
         j = forward_order(i)
-        dp_copy(j).wait_recv()
-        for k in range(1, n_sp):
-            x_copy(tok.at[j, s], j, k).start()
+        for h in range(PIECES):
+            dp_copy(j, h).wait_recv()
+            for k in range(1, n_sp):
+                x_copy(tok.at[j, s], j, k, h).start()
 
     def out_slice(j):
         row = pl.multiple_of(lax.rem(j, boxes_per) * slots, slots)
@@ -165,11 +175,13 @@
 
         for k in range(1, n_sp):
             source = lax.rem(s + n_sp - k, n_sp)
-            pltpu.make_async_remote_copy(
-                src_ref=tok.at[j, source], dst_ref=tok.at[j, source],
-                send_sem=x_send.at[j, k - 1], recv_sem=x_recv.at[j, k - 1],
-                device_id=(p, lax.rem(s + k, n_sp)), device_id_type=MESH,
-            ).wait_recv()
+            for h in range(PIECES):
+                half = piece(tok.at[j, source], h)
+                pltpu.make_async_remote_copy(
+                    src_ref=half, dst_ref=half,
+                    send_sem=x_send.at[j, k - 1, h], recv_sem=x_recv.at[j, k - 1, h],
+                    device_id=(p, source), device_id_type=MESH,
+                ).wait_recv()
 
         def project(c):
             @pl.when(i == 0)
@@ -231,11 +243,12 @@
 
     lax.fori_loop(0, boxes, step, 0)
 
-    for j in range(1, boxes):
-        dp_copy(j).wait_send()
-    for j in range(boxes):
-        for k in range(1, n_sp):
-            x_copy(tok.at[j, s], j, k).wait_send()
+    for h in range(PIECES):
+        for j in range(1, boxes):
+            dp_copy(j, h).wait_send()
+        for j in range(boxes):
+            for k in range(1, n_sp):
+                x_copy(tok.at[j, s], j, k, h).wait_send()
     for i in range(boxes):
         j = own_order(i)
 
@@ -271,19 +284,17 @@
         chunk = 2 * HEAD if kv_cols % (2 * HEAD) == 0 and q_cols % (2 * HEAD) == 0 else HEAD
         chunks = (q_cols + 2 * kv_cols) // chunk
         heads = (q_cols + 2 * kv_cols) // HEAD
-        half = jnp.arange(HEAD // 2, dtype=jnp.float32)
+        half = np.arange(HEAD // 2, dtype=np.float64)
         freq = ROPE_BASE ** (-(half * 2.0 / HEAD))
-        freq = jnp.broadcast_to(jnp.concatenate([freq, freq])[None, :], (8, HEAD))
+        freq = jnp.asarray(np.tile(freq, (8, 2)).astype(np.float32))
         vmem = pl.BlockSpec(memory_space=pltpu.VMEM)
         hbm = pl.BlockSpec(memory_space=pl.ANY)
         dma = pltpu.SemaphoreType.DMA
         return pl.pallas_call(
             functools.partial(kernel, n_dp, n_sp, q_cols // kv_cols, chunk),
-            out_shape=jax.ShapeDtypeStruct(
-                (1, boxes * slots // n_sp, q_cols * n_sp), jnp.bfloat16
-            ),
+            out_shape=pltpu.VMEM((1, boxes * slots // n_sp, q_cols * n_sp), jnp.bfloat16),
             in_specs=[hbm, vmem, vmem, hbm, hbm, hbm],
-            out_specs=hbm,
+            out_specs=vmem,
             scratch_shapes=[
                 pltpu.VMEM((chunks, width, chunk), jnp.bfloat16),
                 pltpu.VMEM((boxes, n_sp, part, width), jnp.bfloat16),
@@ -296,12 +307,12 @@
                 pltpu.VMEM((slots, HEAD), jnp.float32),
                 dma((chunks,)),
                 dma,
+                dma((boxes, PIECES)),
+                dma((boxes, PIECES)),
                 dma((boxes,)),
                 dma((boxes,)),
-                dma((boxes,)),
-                dma((boxes,)),
-                dma((boxes, n_sp - 1)),
-                dma((boxes, n_sp - 1)),
+                dma((boxes, n_sp - 1, PIECES)),
+                dma((boxes, n_sp - 1, PIECES)),
                 dma((boxes,)),
                 dma((boxes // n_sp, n_sp - 1)),
             ],

time: 73.7 us -> 70.3 us (0.954)
  local copies, waits for them, and re-layouts: 3.45 us -> 1.23 us
  Pallas kernels: 69.9 us -> 68.9 us
    unnamed x1, local copies, waits for them, and re-layouts: 2.85 us -> 1.23 us
    pallas_call x1, Pallas kernels: 69.9 us -> 68.9 us  [local(): pl.pallas_call(functools.partial(kernel, n_dp, n_sp, q_cols // kv_cols, c...]
where the time goes in v2:
time: 70.3 us; the launch traced here: 70.1 us
  Pallas kernels  68.9 us (98%)
  local copies, waits for them, and re-layouts  1.23 us (2%)
    pallas_call x1, Pallas kernels, local(): pl.pallas_call(functools.partial(kernel, n_dp, n_sp, q_cols // kv_cols, c...  68.9 us

profile of v2, /device:TPU:0, one launch (start us, length us, event | category | flops | bytes accessed | tf_op | source)
XLA Modules:
  0.0 70.1 jit_solution(7559163220545898682)
XLA Ops:
  0.0 68.9 %rebalanced_attention.1 = bf16[1,256,3584]{2,1,0:T(8,128)(2,1)S(1)} custom-call(bf16[1,4,64,3584]{3,2,1,0:T(8,128)(2,1)} %hidden.1, s32[1,4,128]{2,1,0:T(4,128)} %segs.1, f32[8,128]{1,0:T(8,128)} %constant.2.clone.freq, bf16[3584,1792]{1,0:T(8,128)(2,1)} %w_query.1, bf16[3584,256]{1,0:T(8,128)(2,1)} %w_key.1, bf16[3584,256]{1,0:T(8,128)(2,1)} %w_value.1), custom_call_target="tpu_custom_call" | custom-call | tf_op jit(solution)/shard_map/rebalanced_attention/pallas_call | solution.py:293
  68.9 1.2 %copy.8 = bf16[1,256,3584]{2,1,0:T(8,128)(2,1)} copy(bf16[1,256,3584]{2,1,0:T(8,128)(2,1)S(1)} %rebalanced_attention.1) | data formatting | bytes 3670016

commit v3 on v2

--- a/solution.py
+++ b/solution.py
@@ -16,9 +16,9 @@
 
 def kernel(
     n_dp, n_sp, heads_per_kv, chunk,
-    hidden, segs, freq, w_query, w_key, w_value, out,
-    wbuf, tok, segbuf, qkv, att, cos_ref, sin_ref, bias_ref, live_ref,
-    w_sem, own_sem, dp_send, dp_recv, seg_send, seg_recv, x_send, x_recv,
+    hidden, segs, freq_hbm, w_query, w_key, w_value, out,
+    wbuf, tok, segbuf, qkv, att, cos_ref, sin_ref, bias_ref, live_ref, freq,
+    w_sem, own_sem, own_seg_sem, freq_sem, dp_send, dp_recv, seg_send, seg_recv, x_send, x_recv,
     o_send, o_recv,
 ):
     boxes = hidden.shape[1]
@@ -87,14 +87,19 @@
 
     barrier = pltpu.get_barrier_semaphore()
     for j in range(1, boxes):
-        for q in (lax.rem(p + j, n_dp), lax.rem(p + n_dp - j, n_dp)):
-            pl.semaphore_signal(barrier, inc=1, device_id=(q, s), device_id_type=MESH)
+        pl.semaphore_signal(
+            barrier, inc=1, device_id=(lax.rem(p + n_dp - j, n_dp), s), device_id_type=MESH
+        )
     for k in range(1, n_sp):
         pl.semaphore_signal(
             barrier, inc=1, device_id=(p, lax.rem(s + k, n_sp)), device_id_type=MESH
         )
     own_copy.start()
-    pl.semaphore_wait(barrier, 2 * (boxes - 1) + n_sp - 1)
+    own_segs = pltpu.make_async_copy(segs.at[0], segbuf.at[0], own_seg_sem)
+    freq_copy = pltpu.make_async_copy(freq_hbm, freq, freq_sem)
+    own_segs.start()
+    freq_copy.start()
+    pl.semaphore_wait(barrier, boxes - 1 + n_sp - 1)
 
     for j in range(1, boxes):
         seg_copy(j).start()
@@ -108,7 +113,8 @@
     for c in range(total_chunks):
         weight_copy(c).start()
 
-    segbuf[0] = segs[0]
+    freq_copy.wait()
+    own_segs.wait()
     own_copy.wait()
     for j in range(1, boxes):
         seg_copy(j).wait()
@@ -293,7 +299,7 @@
         return pl.pallas_call(
             functools.partial(kernel, n_dp, n_sp, q_cols // kv_cols, chunk),
             out_shape=pltpu.VMEM((1, boxes * slots // n_sp, q_cols * n_sp), jnp.bfloat16),
-            in_specs=[hbm, vmem, vmem, hbm, hbm, hbm],
+            in_specs=[hbm] * 6,
             out_specs=vmem,
             scratch_shapes=[
                 pltpu.VMEM((chunks, width, chunk), jnp.bfloat16),
@@ -305,7 +311,10 @@
                 pltpu.VMEM((slots, HEAD), jnp.float32),
                 pltpu.VMEM((slots, slots), jnp.float32),
                 pltpu.VMEM((slots, HEAD), jnp.float32),
+                pltpu.VMEM((8, HEAD), jnp.float32),
                 dma((chunks,)),
+                dma,
+                dma,
                 dma,
                 dma((boxes, PIECES)),
                 dma((boxes, PIECES)),

time: 70.3 us -> 67.9 us (0.966)
  Pallas kernels: 68.9 us -> 66.5 us
    pallas_call x1, Pallas kernels: 68.9 us -> 66.5 us  [local(): pl.pallas_call(functools.partial(kernel, n_dp, n_sp, q_cols // kv_cols, c...]
where the time goes in v3:
time: 67.9 us; the launch traced here: 67.7 us
  Pallas kernels  66.5 us (98%)
  local copies, waits for them, and re-layouts  1.23 us (2%)
    pallas_call x1, Pallas kernels, local(): pl.pallas_call(functools.partial(kernel, n_dp, n_sp, q_cols // kv_cols, c...  66.5 us

profile of v3, /device:TPU:0, one launch (start us, length us, event | category | flops | bytes accessed | tf_op | source)
XLA Modules:
  0.0 67.7 jit_solution(7725830951042944281)
XLA Ops:
  0.0 66.5 %rebalanced_attention.1 = bf16[1,256,3584]{2,1,0:T(8,128)(2,1)S(1)} custom-call(bf16[1,4,64,3584]{3,2,1,0:T(8,128)(2,1)} %hidden.1, s32[1,4,128]{2,1,0:T(4,128)} %segs.1, f32[8,128]{1,0:T(8,128)} %constant.2.clone.freq_hbm, bf16[3584,1792]{1,0:T(8,128)(2,1)} %w_query.1, bf16[3584,256]{1,0:T(8,128)(2,1)} %w_key.1, bf16[3584,256]{1,0:T(8,128)(2,1)} %w_value.1), custom_call_target="tpu_custom_call" | custom-call | tf_op jit(solution)/shard_map/rebalanced_attention/pallas_call | solution.py:299
  66.5 1.2 %copy.8 = bf16[1,256,3584]{2,1,0:T(8,128)(2,1)} copy(bf16[1,256,3584]{2,1,0:T(8,128)(2,1)S(1)} %rebalanced_attention.1) | data formatting | bytes 3670016
